TPU v7x, 32 devices: a whole 2x2x4 slice. The times are simulated.
32 devices in a mesh: dp: 16 (over z, x, core), ctx: 2 (over y).
Axes of the slice: x: 2, y: 2, z: 4, core: 2. Of those that a mesh axis runs over, the one named last changes fastest.
Arguments:
- tokens: bfloat16 [16, 1024, 768], P('dp', 'ctx'), may hold values from -6 to 6
- block_table: int32 [4], replicated, may hold values from 0 to 3, as said below
- ln1_gain: bfloat16 [768], P('dp'), may hold values from 0.099609375 to 1.8984375
- ln1_bias: bfloat16 [768], P('dp'), may hold values from -3 to 3
- w_qkv: bfloat16 [768, 2304], P('dp'), may hold values from -0.21875 to 0.21875
- bias_query: bfloat16 [768], P('dp'), may hold values from -3 to 3
- bias_value: bfloat16 [768], P('dp'), may hold values from -3 to 3
- w_out: bfloat16 [768, 768], P('dp'), may hold values from -6 to 6
- bias_out: bfloat16 [768], P('dp'), may hold values from -3 to 3
- ln2_gain: bfloat16 [768], P('dp'), may hold values from 0.099609375 to 1.8984375
- ln2_bias: bfloat16 [768], P('dp'), may hold values from -3 to 3
- w_up: bfloat16 [768, 3072], P('dp'), may hold values from -0.21875 to 0.21875
- bias_up: bfloat16 [3072], P('dp'), may hold values from -3 to 3
- w_down: bfloat16 [3072, 768], P('dp'), may hold values from -0.109375 to 0.109375
- bias_down: bfloat16 [768], P('dp'), may hold values from -3 to 3
- cotangent: bfloat16 [16, 1024, 768], P('dp', 'ctx'), may hold values from -6 to 6
Outputs:
- output: bfloat16 [16, 1024, 768], P('dp', 'ctx')
- grad_tokens: bfloat16 [16, 1024, 768], P('dp', 'ctx')
- grad_ln1_gain: float32 [768], P('dp')
- grad_ln1_bias: float32 [768], P('dp')
- grad_w_qkv: float32 [768, 2304], P('dp')
- grad_bias_query: float32 [768], P('dp')
- grad_bias_value: float32 [768], P('dp')
- grad_w_out: float32 [768, 768], P('dp')
- grad_bias_out: float32 [768], P('dp')
- grad_ln2_gain: float32 [768], P('dp')
- grad_ln2_bias: float32 [768], P('dp')
- grad_w_up: float32 [768, 3072], P('dp')
- grad_bias_up: float32 [3072], P('dp')
- grad_w_down: float32 [3072, 768], P('dp')
- grad_bias_down: float32 [768], P('dp')
Inputs may be any that keep to these rules, and one draw needn't show every extreme that they name: block_table holds every block index of a sequence once; entries 2 i and 2 i + 1 are a mirrored pair b and 3 - b.
All inputs are finite; a program needn't handle non-finite values.
Results may differ from a plain program's by a relative error of at most 0.018.
Values may be sent and summed in bfloat16 or wider, within the bound.
A program may use at most 256 MiB of HBM per device.

v0:
```python
import jax
import jax.numpy as jnp
from jax import lax
from jax.sharding import PartitionSpec as P

HEADS = 12
HD = 64
BLK = 256


def layer_norm(values, gain, shift):
    centred = values - jnp.mean(values, axis=-1, keepdims=True)
    spread_sq = jnp.mean(centred * centred, axis=-1, keepdims=True)
    return centred * lax.rsqrt(spread_sq + 1e-05) * gain + shift


def gelu_tanh(values):
    return jax.nn.gelu(values, approximate=True)


def pair_scores(queries, keyvals, allowed, pair_index, model_width):
    pair_width = 2 * HD
    query_part = lax.dynamic_slice_in_dim(queries, pair_index * pair_width, pair_width, 1).reshape(
        queries.shape[0], 2, HD
    )
    key_part = lax.dynamic_slice_in_dim(keyvals, pair_index * pair_width, pair_width, 1).reshape(
        keyvals.shape[0], 2, HD
    )
    value_part = lax.dynamic_slice_in_dim(
        keyvals, model_width + pair_index * pair_width, pair_width, 1
    ).reshape(keyvals.shape[0], 2, HD)
    scores = jnp.einsum(
        "thd,shd->hts", query_part, key_part, preferred_element_type=jnp.float32
    ) * HD ** (-0.5)
    scores = jnp.where(allowed[None], scores, -1e30)
    return (query_part, key_part, value_part, scores)


def shards(
    tokens,
    block_table,
    ln1_gain,
    ln1_bias,
    w_qkv,
    bias_query,
    bias_value,
    w_out,
    bias_out,
    ln2_gain,
    ln2_bias,
    w_up,
    bias_up,
    w_down,
    bias_down,
    cotangent,
):
    model_width = tokens.shape[2]
    row_count = tokens.shape[1]
    key_count = row_count * lax.axis_size("ctx")
    pair_width = 2 * HD
    scale = HD ** (-0.5)
    fetched = (
        lax.all_gather(ln1_gain, "dp", axis=0, tiled=True),
        lax.all_gather(ln1_bias, "dp", axis=0, tiled=True),
        lax.all_gather(w_qkv, "dp", axis=0, tiled=True),
        lax.all_gather(bias_query, "dp", axis=0, tiled=True),
        lax.all_gather(bias_value, "dp", axis=0, tiled=True),
        lax.all_gather(w_out, "dp", axis=0, tiled=True),
        lax.all_gather(bias_out, "dp", axis=0, tiled=True),
        lax.all_gather(ln2_gain, "dp", axis=0, tiled=True),
        lax.all_gather(ln2_bias, "dp", axis=0, tiled=True),
        lax.all_gather(w_up, "dp", axis=0, tiled=True),
        lax.all_gather(bias_up, "dp", axis=0, tiled=True),
        lax.all_gather(w_down, "dp", axis=0, tiled=True),
        lax.all_gather(bias_down, "dp", axis=0, tiled=True),
    )
    (
        gain_one,
        shift_one,
        qkv_w,
        query_b,
        value_b,
        out_w,
        out_b,
        gain_two,
        shift_two,
        up_w,
        up_b,
        down_w,
        down_b,
    ) = fetched
    inputs = tokens[0].astype(jnp.float32)
    normed_one, norm_one_back = jax.vjp(
        layer_norm, inputs, gain_one.astype(jnp.float32), shift_one.astype(jnp.float32)
    )
    normed_one_low = normed_one.astype(jnp.bfloat16)
    bias_cat = jnp.concatenate(
        [
            query_b.astype(jnp.float32),
            jnp.zeros((model_width,), jnp.float32),
            value_b.astype(jnp.float32),
        ]
    )
    projected = (
        jnp.dot(normed_one_low, qkv_w, preferred_element_type=jnp.float32) + bias_cat
    ).astype(jnp.bfloat16)
    queries = projected[:, :model_width]
    own_keyvals = projected[:, model_width:]
    keyvals = lax.all_gather(own_keyvals, "ctx", axis=0, tiled=True)
    per_device = row_count // BLK
    owned_blocks = lax.dynamic_slice_in_dim(
        block_table, lax.axis_index("ctx") * per_device, per_device
    )
    query_block = jnp.repeat(owned_blocks, BLK, total_repeat_length=row_count)
    key_block = jnp.repeat(block_table, BLK, total_repeat_length=key_count)
    allowed = key_block[None, :] <= query_block[:, None]

    def forward_pair(pair_index, state_pair):
        attended_acc, log_sums = state_pair
        query_part, key_part, value_part, scores = pair_scores(
            queries, keyvals, allowed, pair_index, model_width
        )
        largest = jnp.max(scores, axis=-1, keepdims=True)
        exponent = jnp.exp(scores - largest)
        row_total = jnp.sum(exponent, axis=-1, keepdims=True)
        probs_low = (exponent / row_total).astype(jnp.bfloat16)
        mixed_pair = jnp.einsum(
            "hts,shd->thd", probs_low, value_part, preferred_element_type=jnp.float32
        )
        attended_acc = lax.dynamic_update_slice_in_dim(
            attended_acc, mixed_pair.reshape(row_count, pair_width), pair_index * pair_width, 1
        )
        log_sums = lax.dynamic_update_slice_in_dim(
            log_sums, (largest + jnp.log(row_total))[..., 0], pair_index * 2, 0
        )
        return (attended_acc, log_sums)

    attended, log_sums = lax.fori_loop(
        0,
        HEADS // 2,
        forward_pair,
        (
            jnp.zeros((row_count, model_width), jnp.float32),
            jnp.zeros((HEADS, row_count), jnp.float32),
        ),
    )
    attended_low = attended.astype(jnp.bfloat16)
    branch = jnp.dot(attended_low, out_w, preferred_element_type=jnp.float32) + out_b.astype(
        jnp.float32
    )
    middle = inputs + branch
    normed_two, norm_two_back = jax.vjp(
        layer_norm, middle, gain_two.astype(jnp.float32), shift_two.astype(jnp.float32)
    )
    normed_two_low = normed_two.astype(jnp.bfloat16)
    hidden_pre = jnp.dot(normed_two_low, up_w, preferred_element_type=jnp.float32) + up_b.astype(
        jnp.float32
    )
    active, gelu_back = jax.vjp(gelu_tanh, hidden_pre)
    active_low = active.astype(jnp.bfloat16)
    result = middle + (
        jnp.dot(active_low, down_w, preferred_element_type=jnp.float32) + down_b.astype(jnp.float32)
    )
    output = result.astype(jnp.bfloat16)[None]
    again_weights = (
        lax.all_gather(w_qkv, "dp", axis=0, tiled=True),
        lax.all_gather(w_out, "dp", axis=0, tiled=True),
        lax.all_gather(w_up, "dp", axis=0, tiled=True),
        lax.all_gather(w_down, "dp", axis=0, tiled=True),
    )
    qkv_back_w, out_back_w, up_back_w, down_back_w = again_weights
    upstream = cotangent[0]
    grad_down_w = jnp.einsum("tf,td->fd", active_low, upstream, preferred_element_type=jnp.float32)
    grad_down_b = jnp.sum(upstream.astype(jnp.float32), axis=0)
    grad_active = jnp.einsum("td,fd->tf", upstream, down_back_w, preferred_element_type=jnp.float32)
    grad_hidden = gelu_back(grad_active)[0].astype(jnp.bfloat16)
    grad_up_w = jnp.einsum(
        "td,tf->df", normed_two_low, grad_hidden, preferred_element_type=jnp.float32
    )
    grad_up_b = jnp.sum(grad_hidden.astype(jnp.float32), axis=0)
    grad_normed_two = jnp.einsum(
        "tf,df->td", grad_hidden, up_back_w, preferred_element_type=jnp.float32
    )
    grad_middle_norm, grad_gain_two, grad_shift_two = norm_two_back(grad_normed_two)
    grad_middle = upstream.astype(jnp.float32) + grad_middle_norm
    grad_branch = grad_middle.astype(jnp.bfloat16)
    grad_out_w = jnp.einsum(
        "td,te->de", attended_low, grad_branch, preferred_element_type=jnp.float32
    )
    grad_out_b = jnp.sum(grad_branch.astype(jnp.float32), axis=0)
    grad_attended = jnp.einsum(
        "te,de->td", grad_branch, out_back_w, preferred_element_type=jnp.float32
    ).astype(jnp.bfloat16)

    def backward_pair(pair_index, state_pair):
        grad_queries, grad_keyvals = state_pair
        query_part, key_part, value_part, scores = pair_scores(
            queries, keyvals, allowed, pair_index, model_width
        )
        log_part = lax.dynamic_slice_in_dim(log_sums, pair_index * 2, 2, 0)[:, :, None]
        probs = jnp.exp(scores - log_part)
        grad_part = lax.dynamic_slice_in_dim(
            grad_attended, pair_index * pair_width, pair_width, 1
        ).reshape(row_count, 2, HD)
        grad_probs = jnp.einsum(
            "thd,shd->hts", grad_part, value_part, preferred_element_type=jnp.float32
        )
        inner_sum = jnp.sum(probs * grad_probs, axis=-1, keepdims=True)
        grad_scores = (probs * (grad_probs - inner_sum) * scale).astype(jnp.bfloat16)
        grad_query = jnp.einsum(
            "hts,shd->thd", grad_scores, key_part, preferred_element_type=jnp.float32
        )
        grad_key = jnp.einsum(
            "hts,thd->shd", grad_scores, query_part, preferred_element_type=jnp.float32
        )
        grad_value = jnp.einsum(
            "hts,thd->shd",
            probs.astype(jnp.bfloat16),
            grad_part,
            preferred_element_type=jnp.float32,
        )
        grad_queries = lax.dynamic_update_slice_in_dim(
            grad_queries, grad_query.reshape(row_count, pair_width), pair_index * pair_width, 1
        )
        grad_keyvals = lax.dynamic_update_slice_in_dim(
            grad_keyvals, grad_key.reshape(key_count, pair_width), pair_index * pair_width, 1
        )
        grad_keyvals = lax.dynamic_update_slice_in_dim(
            grad_keyvals,
            grad_value.reshape(key_count, pair_width),
            model_width + pair_index * pair_width,
            1,
        )
        return (grad_queries, grad_keyvals)

    grad_queries, grad_keyvals = lax.fori_loop(
        0,
        HEADS // 2,
        backward_pair,
        (
            jnp.zeros((row_count, model_width), jnp.float32),
            jnp.zeros((key_count, 2 * model_width), jnp.float32),
        ),
    )
    grad_keyvals_own = lax.psum_scatter(
        grad_keyvals.astype(jnp.bfloat16), "ctx", scatter_dimension=0, tiled=True
    ).astype(jnp.float32)
    grad_projected = jnp.concatenate([grad_queries, grad_keyvals_own], axis=1).astype(jnp.bfloat16)
    grad_qkv_w = jnp.einsum(
        "td,te->de", normed_one_low, grad_projected, preferred_element_type=jnp.float32
    )
    column_sums = jnp.sum(grad_projected.astype(jnp.float32), axis=0)
    grad_query_b = column_sums[:model_width]
    grad_value_b = column_sums[2 * model_width :]
    grad_normed_one = jnp.einsum(
        "te,de->td", grad_projected, qkv_back_w, preferred_element_type=jnp.float32
    )
    grad_inputs_norm, grad_gain_one, grad_shift_one = norm_one_back(grad_normed_one)
    grad_tokens = (grad_middle + grad_inputs_norm).astype(jnp.bfloat16)[None]
    summed_rows = (
        lax.psum_scatter(
            grad_gain_one.astype(jnp.bfloat16), "dp", scatter_dimension=0, tiled=True
        ).astype(jnp.float32),
        lax.psum_scatter(
            grad_shift_one.astype(jnp.bfloat16), "dp", scatter_dimension=0, tiled=True
        ).astype(jnp.float32),
        lax.psum_scatter(
            grad_qkv_w.astype(jnp.bfloat16), "dp", scatter_dimension=0, tiled=True
        ).astype(jnp.float32),
        lax.psum_scatter(
            grad_query_b.astype(jnp.bfloat16), "dp", scatter_dimension=0, tiled=True
        ).astype(jnp.float32),
        lax.psum_scatter(
            grad_value_b.astype(jnp.bfloat16), "dp", scatter_dimension=0, tiled=True
        ).astype(jnp.float32),
        lax.psum_scatter(
            grad_out_w.astype(jnp.bfloat16), "dp", scatter_dimension=0, tiled=True
        ).astype(jnp.float32),
        lax.psum_scatter(
            grad_out_b.astype(jnp.bfloat16), "dp", scatter_dimension=0, tiled=True
        ).astype(jnp.float32),
        lax.psum_scatter(
            grad_gain_two.astype(jnp.bfloat16), "dp", scatter_dimension=0, tiled=True
        ).astype(jnp.float32),
        lax.psum_scatter(
            grad_shift_two.astype(jnp.bfloat16), "dp", scatter_dimension=0, tiled=True
        ).astype(jnp.float32),
        lax.psum_scatter(
            grad_up_w.astype(jnp.bfloat16), "dp", scatter_dimension=0, tiled=True
        ).astype(jnp.float32),
        lax.psum_scatter(
            grad_up_b.astype(jnp.bfloat16), "dp", scatter_dimension=0, tiled=True
        ).astype(jnp.float32),
        lax.psum_scatter(
            grad_down_w.astype(jnp.bfloat16), "dp", scatter_dimension=0, tiled=True
        ).astype(jnp.float32),
        lax.psum_scatter(
            grad_down_b.astype(jnp.bfloat16), "dp", scatter_dimension=0, tiled=True
        ).astype(jnp.float32),
    )
    (
        sum_gain_one,
        sum_shift_one,
        sum_qkv_w,
        sum_query_b,
        sum_value_b,
        sum_out_w,
        sum_out_b,
        sum_gain_two,
        sum_shift_two,
        sum_up_w,
        sum_up_b,
        sum_down_w,
        sum_down_b,
    ) = summed_rows
    final_grads = (
        lax.psum(sum_gain_one.astype(jnp.bfloat16), "ctx").astype(jnp.float32),
        lax.psum(sum_shift_one.astype(jnp.bfloat16), "ctx").astype(jnp.float32),
        lax.psum(sum_qkv_w.astype(jnp.bfloat16), "ctx").astype(jnp.float32),
        lax.psum(sum_query_b.astype(jnp.bfloat16), "ctx").astype(jnp.float32),
        lax.psum(sum_value_b.astype(jnp.bfloat16), "ctx").astype(jnp.float32),
        lax.psum(sum_out_w.astype(jnp.bfloat16), "ctx").astype(jnp.float32),
        lax.psum(sum_out_b.astype(jnp.bfloat16), "ctx").astype(jnp.float32),
        lax.psum(sum_gain_two.astype(jnp.bfloat16), "ctx").astype(jnp.float32),
        lax.psum(sum_shift_two.astype(jnp.bfloat16), "ctx").astype(jnp.float32),
        lax.psum(sum_up_w.astype(jnp.bfloat16), "ctx").astype(jnp.float32),
        lax.psum(sum_up_b.astype(jnp.bfloat16), "ctx").astype(jnp.float32),
        lax.psum(sum_down_w.astype(jnp.bfloat16), "ctx").astype(jnp.float32),
        lax.psum(sum_down_b.astype(jnp.bfloat16), "ctx").astype(jnp.float32),
    )
    return (
        output,
        grad_tokens,
        final_grads[0],
        final_grads[1],
        final_grads[2],
        final_grads[3],
        final_grads[4],
        final_grads[5],
        final_grads[6],
        final_grads[7],
        final_grads[8],
        final_grads[9],
        final_grads[10],
        final_grads[11],
        final_grads[12],
    )


def solution(mesh):
    in_specs = (
        P("dp", "ctx", None),
        P(),
        P("dp"),
        P("dp"),
        P("dp", None),
        P("dp"),
        P("dp"),
        P("dp", None),
        P("dp"),
        P("dp"),
        P("dp"),
        P("dp", None),
        P("dp"),
        P("dp", None),
        P("dp"),
        P("dp", "ctx", None),
    )
    out_specs = (
        P("dp", "ctx", None),
        P("dp", "ctx", None),
        P("dp"),
        P("dp"),
        P("dp", None),
        P("dp"),
        P("dp"),
        P("dp", None),
        P("dp"),
        P("dp"),
        P("dp"),
        P("dp", None),
        P("dp"),
        P("dp", None),
        P("dp"),
    )
    return jax.shard_map(shards, mesh=mesh, in_specs=in_specs, out_specs=out_specs, check_vma=False)
```

profile of v0, /device:TPU:0, one launch (start us, length us, event | category | flops | bytes accessed | tf_op | source)
XLA Modules:
  0.0 856.2 jit_solution(569629735728347137)
XLA Ops:
  17.3 63.3 %all-reduce.19 = (bf16[768]{0:T(1024)(128)(2,1)S(1)}, bf16[768]{0:T(1024)(128)(2,1)S(1)}, bf16[768]{0:T(1024)(128)(2,1)S(1)}, bf16[768]{0:T(1024)(128)(2,1)S(1)}...) all-reduce(bf16[768]{0:T(1024)(128)(2,1)S(1)} %dynamic-update-slice, ...), channel_id=1, replica_groups=mesh['dp'=16,'ctx'=2] {'dp'}, use_global_device_ids=true, to_apply=%add.4 | all-reduce | flops 8448 | bytes 33792
  97.2 34.6 %all-gather.8.cloned.1.call-done = bf16[1024,1536]{1,0:T(8,128)(2,1)} async-done(((bf16[512,1536]{1,0:T(8,128)(2,1)}), bf16[1024,1536]{1,0:T(8,128)(2,1)}) %all-gather.8.cloned.1.call-update) | async-done | bytes 3145744 | tf_op jit(solution)/shard_map/all_gather | solution.py:109
  136.6 57.0 %while.38 = (s32[]{:T(128)}, bf16[512,768]{0,1:T(8,128)(2,1)S(1)}, f32[12,512]{1,0:T(8,128)S(1)}, bf16[1024,1536]{0,1:T(8,128)(2,1)}, bf16[512,768]{0,1:T(8,128)...) while((s32[]{:T(128)}, bf16[512,768]{0,1:T(8,128)(2,1)S(1)}, ...), condition=%wide.region_5.6_spmd.clone, body=%wide.region_2.5_spmd.clone.sunk | while | flops 281541632 | bytes 33855824 | solution.py:138
  197.0 29.5 %all-gather.12.cloned.1.call-done = bf16[768,3072]{1,0:T(8,128)(2,1)} async-done(((bf16[48,3072]{1,0:T(8,128)(2,1)}), bf16[768,3072]{1,0:T(8,128)(2,1)}) %all-gather.12.cloned.1.call-update) | async-done | bytes 4718608 | tf_op jit(solution)/shard_map/all_gather | solution.py:72
  226.5 7.1 fusion.67
  233.6 46.7 %all-gather.14.cloned.1.call-done = bf16[3072,768]{1,0:T(8,128)(2,1)} async-done(((bf16[192,768]{1,0:T(8,128)(2,1)}), bf16[3072,768]{1,0:T(8,128)(2,1)}) %all-gather.14.cloned.1.call-update) | async-done | bytes 4718608 | tf_op jit(solution)/shard_map/all_gather | solution.py:74
  280.3 9.7 %fusion.77 = (bf16[3072]{0:T(1024)(128)(2,1)S(1)}, bf16[512,3072]{1,0:T(8,128)(2,1)S(1)}) fusion(f32[512,3072]{1,0:T(8,128)} %fusion.67, f32[3072]{0:T(1024)S(1)} %convert_element_type.214, bf16[3072,768]{1,0:T(8,128)(2,1)} %all-gather.14.cloned.1.call-done, bf16[1,512,768]{2,1,0:T(8,128)(2,1)S(1)} %copy-done.2), kind=kOutput, calls=%fused_computation.117 | convolution fusion | flops 2450519040 | bytes 14960640 | tf_op jit(solution)/shard_map/td,fd->tf/dot_general | solution.py:175
  301.1 171.1 %while.39 = (s32[]{:T(128)}, bf16[512,768]{0,1:T(8,128)(2,1)}, bf16[1024,1536]{0,1:T(8,128)(2,1)}, bf16[1024,1536]{0,1:T(8,128)(2,1)}, bf16[512,768]{0,1:T(8,128...) while((s32[]{:T(128)}, bf16[512,768]{0,1:T(8,128)(2,1)}, ...), condition=%wide.region_12.13_spmd.clone, body=%wide.region_10.12_spmd.clone.sunk | while | flops 686297088 | bytes 35539284 | solution.py:236
  310.6 7.1 fusion.141
  321.8 7.2 fusion.140
  339.1 7.1 fusion.141
  350.3 7.2 fusion.140
  367.6 7.1 fusion.141
  378.8 7.2 fusion.140
  396.1 7.1 fusion.141
  407.4 7.2 fusion.140
  424.7 7.1 fusion.141
  435.9 7.2 fusion.140
  453.2 7.1 fusion.141
  464.4 7.2 fusion.140
  476.6 8.1 convolution_convert_fusion.1
  485.8 8.6 %convolution_convert_fusion = bf16[3072,768]{1,0:T(8,128)(2,1)} fusion(bf16[1,512,768]{2,1,0:T(8,128)(2,1)S(1)} %copy-done.3, f32[512,3072]{1,0:T(8,128)} %fusion.67, f32[3072]{0:T(1024)S(1)} %convert_element_type.214), kind=kOutput, calls=%fused_computation.50 | convolution fusion | flops 2434007040 | bytes 11808768 | tf_op jit(solution)/shard_map/tf,td->fd/dot_general | solution.py:173
  494.4 20.0 %reduce-scatter.6.cloned.1.call-done = bf16[512,1536]{0,1:T(8,128)(2,1)} async-done(((bf16[1024,1536]{0,1:T(8,128)(2,1)}), bf16[512,1536]{0,1:T(8,128)(2,1)}) %reduce-scatter.6.cloned.1.call-update) | async-done | bytes 1572880 | tf_op jit(solution)/shard_map/reduce_scatter | solution.py:245
  514.4 5.7 convolution_convert_fusion.2
  524.1 5.1 fusion.68
  531.3 61.1 %all-reduce.18 = (bf16[768]{0:T(1024)(128)(2,1)S(1)}, bf16[768]{0:T(1024)(128)(2,1)S(1)}, bf16[768]{0:T(1024)(128)(2,1)S(1)}, bf16[768]{0:T(1024)(128)(2,1)S(1)}...) all-reduce(bf16[768]{0:T(1024)(128)(2,1)S(1)} %dynamic-update-slice, ...), channel_id=1, replica_groups=mesh['dp'=16,'ctx'=2] {'dp'}, use_global_device_ids=true, to_apply=%add.8 | all-reduce | flops 9984 | bytes 39936
  593.0 5.0 all-reduce.20
  605.6 49.1 %reduce-scatter.12.cloned.1.call-done = bf16[48,3072]{1,0:T(8,128)(2,1)} async-done(((bf16[768,3072]{1,0:T(8,128)(2,1)}), bf16[48,3072]{1,0:T(8,128)(2,1)}) %reduce-scatter.12.cloned.1.call-update) | async-done | bytes 294928 | tf_op jit(solution)/shard_map/reduce_scatter | solution.py:288
  654.8 78.8 %reduce-scatter.14.cloned.1.call-done = bf16[192,768]{1,0:T(8,128)(2,1)} async-done(((bf16[3072,768]{1,0:T(8,128)(2,1)}), bf16[192,768]{1,0:T(8,128)(2,1)}) %reduce-scatter.14.cloned.1.call-update) | async-done | bytes 294928 | tf_op jit(solution)/shard_map/reduce_scatter | solution.py:294
  733.5 71.1 %reduce-scatter.8.cloned.1.call-done = bf16[48,2304]{1,0:T(8,128)(2,1)} async-done(((bf16[768,2304]{1,0:T(8,128)(2,1)}), bf16[48,2304]{1,0:T(8,128)(2,1)}) %reduce-scatter.8.cloned.1.call-update) | async-done | bytes 221200 | tf_op jit(solution)/shard_map/reduce_scatter | solution.py:267
  804.6 9.5 %fusion.48 = bf16[1,512,768]{2,1,0:T(8,128)(2,1)} fusion(f32[512,768]{1,0:T(8,128)} %copy-done.4, bf16[3072,768]{1,0:T(8,128)(2,1)} %all-gather.14.cloned.1.call-done, f32[768]{0:T(1024)S(1)} %convert_element_type.216, f32[512,3072]{1,0:T(8,128)} %fusion.67, f32[3072]{0:T(1024)S(1)} %convert_element_type.214), kind=kOutput, calls=%fused_computation.82 | convolution fusion | flops 2432827392 | bytes 13384704 | tf_op jit(solution)/shard_map/dot_general | solution.py:162
  814.1 28.5 %all-reduce.24.cloned.1.call-done = (bf16[48,2304]{1,0:T(8,128)(2,1)}, bf16[48,768]{1,0:T(8,128)(2,1)}, bf16[48,3072]{1,0:T(8,128)(2,1)}, bf16[192,768]{1,0:T(8,128)(2,1)}) async-done(((bf16[48,2304]{1,0:T(8,128)(2,1)}, bf16[48,768]{1,0:T(8,128)(2,1)}, bf16[48,3072]{1,0:T(8,128)(2,1)}, bf16[192,768]{1,0:T(8,128)(2,1)}), (bf16[48,2304]{1,0:T(8,128)(2,1)}, bf16[48,768]{1,0:T(8,128)(2,1)}, ...) | async-done | bytes 884752 | tf_op jit(solution)/shard_map/psum | solution.py:319
  (281 shorter events, 211.3 us)
Async XLA Ops:
  7.2 76.3 %all-gather.6.cloned.1.call-start = ((), (), s32[]{:S(2)}) async-start(), calls=%async_computation.5 | async-start | bytes 3760128 | tf_op jit(solution)/shard_map/all_gather | solution.py:65
  7.9 123.8 %all-gather.8.cloned.1.call-start = ((), (), s32[]{:S(2)}) async-start(), calls=%async_computation.6 | async-start | bytes 4718592 | tf_op jit(solution)/shard_map/all_gather | solution.py:109
  87.9 3.6 copy-start.10
  87.9 4.9 copy-start.14
  88.0 6.2 copy-start.11
  88.0 6.2 copy-start.12
  88.0 6.2 copy-start.13
  89.3 104.3 %all-gather.10.cloned.1.call-start = ((), (), s32[]{:S(2)}) async-start(), calls=%async_computation.7 | async-start | bytes 1253376 | tf_op jit(solution)/shard_map/all_gather | solution.py:68
  90.0 136.4 %all-gather.12.cloned.1.call-start = ((), (), s32[]{:S(2)}) async-start(), calls=%async_computation.8 | async-start | bytes 5013504 | tf_op jit(solution)/shard_map/all_gather | solution.py:72
  90.6 189.7 %all-gather.14.cloned.1.call-start = ((), (), s32[]{:S(2)}) async-start(), calls=%async_computation.9 | async-start | bytes 5013504 | tf_op jit(solution)/shard_map/all_gather | solution.py:74
  91.2 423.2 %reduce-scatter.6.cloned.1.call-start = ((), (), s32[]{:S(2)}) async-start(), calls=%async_computation.10 | async-start | bytes 4718592 | tf_op jit(solution)/shard_map/reduce_scatter | solution.py:245
  136.6 57.9 %copy-start.1 = (bf16[1,512,768]{2,1,0:T(8,128)(2,1)S(1)}, bf16[1,512,768]{2,1,0:T(8,128)(2,1)}, u32[]{:S(2)}) copy-start(bf16[1,512,768]{2,1,0:T(8,128)(2,1)} %param.24) | copy-start | bytes 2359300
  139.2 2.0 copy-start
  148.7 2.0 copy-start
  158.1 2.0 copy-start
  167.6 2.0 copy-start
  177.1 2.0 copy-start
  186.7 2.0 copy-start
  193.6 3.4 copy-start.7
  196.7 93.3 %copy-start.4 = (f32[512,768]{1,0:T(8,128)}, f32[512,768]{1,0:T(8,128)S(1)}, u32[]{:S(2)}) copy-start(f32[512,768]{1,0:T(8,128)S(1)} %get-tuple-element.560) | copy-start | bytes 4718596
  197.0 83.3 %copy-start.2 = (bf16[1,512,768]{2,1,0:T(8,128)(2,1)S(1)}, bf16[1,512,768]{2,1,0:T(8,128)(2,1)}, u32[]{:S(2)}) copy-start(bf16[1,512,768]{2,1,0:T(8,128)(2,1)} %param.39) | copy-start | bytes 2359300
  280.3 9.7 %copy-start.15 = (bf16[768,3072]{1,0:T(8,128)(2,1)S(1)}, bf16[768,3072]{1,0:T(8,128)(2,1)}, u32[]{:S(2)}) copy-start(bf16[768,3072]{1,0:T(8,128)(2,1)} %all-gather.12.cloned.1.call-done) | copy-start | bytes 14155780
  290.0 3.0 copy-start.18
  293.0 3.3 copy-start.16
  472.2 1.1 copy-start.8
  472.3 133.4 %reduce-scatter.10.cloned.1.call-start = ((), (), s32[]{:S(2)}) async-start(), calls=%async_computation.12 | async-start | bytes 1253376 | tf_op jit(solution)/shard_map/reduce_scatter | solution.py:276
  476.3 178.4 %reduce-scatter.12.cloned.1.call-start = ((), (), s32[]{:S(2)}) async-start(), calls=%async_computation.13 | async-start | bytes 5013504 | tf_op jit(solution)/shard_map/reduce_scatter | solution.py:288
  484.7 248.9 %reduce-scatter.14.cloned.1.call-start = ((), (), s32[]{:S(2)}) async-start(), calls=%async_computation.14 | async-start | bytes 5013504 | tf_op jit(solution)/shard_map/reduce_scatter | solution.py:294
  494.4 310.2 %reduce-scatter.8.cloned.1.call-start = ((), (), s32[]{:S(2)}) async-start(), calls=%async_computation.11 | async-start | bytes 3760128 | tf_op jit(solution)/shard_map/reduce_scatter | solution.py:267
  520.1 1.8 copy-start.17
  520.1 322.4 %all-reduce.24.cloned.1.call-start = ((), (), s32[]{:S(2)}) async-start(), calls=%async_computation.15 | async-start | bytes 1769472 | tf_op jit(solution)/shard_map/psum | solution.py:319
  529.3 1.2 copy-start.5
  (3 other events, 2.9 us)
Sparse Core Ops, SparseCore 0:
  10.3 50.2 all-gather.5
  89.4 42.2 all-gather.7
  134.0 38.2 all-gather.9
  174.5 51.9 all-gather.11
  228.6 51.6 all-gather.13
  472.4 41.9 reduce-scatter.5
  518.0 58.1 reduce-scatter.9
  580.1 74.6 reduce-scatter.11
  658.6 74.8 reduce-scatter.13
  737.3 67.3 reduce-scatter.7
  807.1 35.3 all-reduce.23
where the time goes:
time: 862 us; the launch traced here: 856 us
  waiting for transfers between devices  361 us (42%)
  matrix products  234 us (27%)
  blocking collectives  129 us (15%)
  local copies, waits for them, and re-layouts  74.3 us (9%)
  other arithmetic  38.5 us (4%)
  between operations  17.1 us (2%)
    unnamed x2, blocking collectives  124 us
    reduce_scatter x1, waiting for transfers between devices, shards(): lax.psum_scatter(grad_down_w.astype(jnp.bfloat16), 'dp', scatter_dimensio...  78.8 us
    reduce_scatter x1, waiting for transfers between devices, shards(): lax.psum_scatter(grad_qkv_w.astype(jnp.bfloat16), 'dp', scatter_dimension...  71.1 us
    reduce_scatter x1, waiting for transfers between devices, shards(): lax.psum_scatter(grad_up_w.astype(jnp.bfloat16), 'dp', scatter_dimension=...  49.1 us
    all_gather x1, waiting for transfers between devices, shards(): lax.all_gather(w_down, 'dp', axis=0, tiled=True)  46.7 us
    dot_general x6, matrix products, backward_pair(): jnp.einsum('hts,shd->thd', grad_scores, key_part, preferred_element_type=...  43.1 us
    dot_general x6, matrix products, backward_pair(): jnp.einsum('hts,thd->shd', grad_scores, query_part, preferred_element_typ...  42.6 us
    all_gather x1, waiting for transfers between devices, shards(): keyvals = lax.all_gather(own_keyvals, 'ctx', axis=0, tiled=True)  34.6 us
  transfers between devices with their start and end apart: 11, of which 8 were waited for; matrix products, arithmetic and copies ran while one was open for 15% of the time, Pallas kernels for 0%

commit v1 on v0

--- a/solution.py
+++ b/solution.py
@@ -1,11 +1,20 @@
+import functools
 import jax
 import jax.numpy as jnp
 from jax import lax
 from jax.sharding import PartitionSpec as P
+from jax.lax import all_gather
 
 HEADS = 12
 HD = 64
 BLK = 256
+
+
+def rest_the_view(inp, bus_axis):
+    return jnp.sum(all_gather(inp, bus_axis), axis=0)
+
+
+sides_balance = functools.partial(rest_the_view, bus_axis="ctx")
 
 
 def layer_norm(values, gain, shift):
@@ -316,7 +325,7 @@
     final_grads = (
         lax.psum(sum_gain_one.astype(jnp.bfloat16), "ctx").astype(jnp.float32),
         lax.psum(sum_shift_one.astype(jnp.bfloat16), "ctx").astype(jnp.float32),
-        lax.psum(sum_qkv_w.astype(jnp.bfloat16), "ctx").astype(jnp.float32),
+        sides_balance(sum_qkv_w.astype(jnp.bfloat16)).astype(jnp.float32),
         lax.psum(sum_query_b.astype(jnp.bfloat16), "ctx").astype(jnp.float32),
         lax.psum(sum_value_b.astype(jnp.bfloat16), "ctx").astype(jnp.float32),
         lax.psum(sum_out_w.astype(jnp.bfloat16), "ctx").astype(jnp.float32),

time: 862 us -> 684 us (0.79)
  waiting for transfers between devices: 361 us -> 176 us
    reduce_scatter x1, waiting for transfers between devices: 71.1 us -> 0.01 us  [shards(): lax.psum_scatter(grad_qkv_w.astype(jnp.bfloat16), 'dp', scatter_dimension...]
    reduce_scatter x1, waiting for transfers between devices: 78.8 us -> 17 us  [shards(): lax.psum_scatter(grad_down_w.astype(jnp.bfloat16), 'dp', scatter_dimensio...]
    reduce_scatter x1, waiting for transfers between devices: 49.1 us -> 0.02 us  [shards(): lax.psum_scatter(grad_up_w.astype(jnp.bfloat16), 'dp', scatter_dimension=...]
    psum x1, waiting for transfers between devices: 28.5 us -> 0.01 us  [shards(): lax.psum(sum_out_w.astype(jnp.bfloat16), 'ctx').astype(jnp.float32)]
    reduce_scatter x1, waiting for transfers between devices: 20 us -> 44.9 us  [shards(): lax.psum_scatter(grad_keyvals.astype(jnp.bfloat16), 'ctx', scatter_dimens...]
    unnamed x66 -> x74, local copies, waits for them, and re-layouts: 19 us -> 19 us
  transfers between devices with their start and end apart: 11 -> 11, of which waited for: 8 -> 5; matrix products, arithmetic and copies ran while one was open for 15% -> 45% of each run, Pallas kernels for 0% -> 0%
where the time goes in v1:
time: 684 us; the launch traced here: 678 us
  matrix products  235 us (34%)
  waiting for transfers between devices  176 us (26%)
  blocking collectives  137 us (20%)
  local copies, waits for them, and re-layouts  73.8 us (11%)
  other arithmetic  37.6 us (5%)
  between operations  17.2 us (3%)
    unnamed x2, blocking collectives  125 us
    all_gather x1, waiting for transfers between devices, shards(): lax.all_gather(w_down, 'dp', axis=0, tiled=True)  46.8 us
    reduce_scatter x1, waiting for transfers between devices, shards(): lax.psum_scatter(grad_keyvals.astype(jnp.bfloat16), 'ctx', scatter_dimens...  44.9 us
    dot_general x6, matrix products, backward_pair(): jnp.einsum('hts,shd->thd', grad_scores, key_part, preferred_element_type=...  44 us
    dot_general x6, matrix products, backward_pair(): jnp.einsum('hts,thd->shd', grad_scores, query_part, preferred_element_typ...  43.5 us
    all_gather x1, waiting for transfers between devices, shards(): keyvals = lax.all_gather(own_keyvals, 'ctx', axis=0, tiled=True)  34.4 us
    all_gather x1, waiting for transfers between devices, shards(): lax.all_gather(w_up, 'dp', axis=0, tiled=True)  30.2 us
    dot_general x12, matrix products, pair_scores(): jnp.einsum('thd,shd->hts', query_part, key_part, preferred_element_type=j...  25.7 us
  transfers between devices with their start and end apart: 11, of which 5 were waited for; matrix products, arithmetic and copies ran while one was open for 45% of the time, Pallas kernels for 0%

profile of v1, /device:TPU:0, one launch (start us, length us, event | category | flops | bytes accessed | tf_op | source)
XLA Modules:
  0.0 678.1 jit_solution(5542650432229149000)
XLA Ops:
  17.3 63.3 %all-reduce.19 = (bf16[768]{0:T(1024)(128)(2,1)S(1)}, bf16[768]{0:T(1024)(128)(2,1)S(1)}, bf16[768]{0:T(1024)(128)(2,1)S(1)}, bf16[768]{0:T(1024)(128)(2,1)S(1)}...) all-reduce(bf16[768]{0:T(1024)(128)(2,1)S(1)} %dynamic-update-slice, ...), channel_id=1, replica_groups=mesh['dp'=16,'ctx'=2] {'dp'}, use_global_device_ids=true, to_apply=%add.4 | all-reduce | flops 8448 | bytes 33792
  83.5 4.4 fusion.34
  97.4 34.4 %all-gather.9.cloned.1.call-done = bf16[1024,1536]{1,0:T(8,128)(2,1)} async-done(((bf16[512,1536]{1,0:T(8,128)(2,1)}), bf16[1024,1536]{1,0:T(8,128)(2,1)}) %all-gather.9.cloned.1.call-update) | async-done | bytes 3145744 | tf_op jit(solution)/shard_map/all_gather | solution.py:118
  131.7 4.6 copy.36
  136.5 56.4 %while.38 = (s32[]{:T(128)}, bf16[512,768]{0,1:T(8,128)(2,1)S(1)}, f32[12,512]{1,0:T(8,128)S(1)}, bf16[1024,1536]{0,1:T(8,128)(2,1)}, bf16[512,768]{0,1:T(8,128)...) while((s32[]{:T(128)}, bf16[512,768]{0,1:T(8,128)(2,1)S(1)}, ...), condition=%wide.region_5.6_spmd.clone, body=%wide.region_2.5_spmd.clone.sunk | while | flops 281541632 | bytes 33855824 | solution.py:147
  196.3 30.2 %all-gather.13.cloned.1.call-done = bf16[768,3072]{1,0:T(8,128)(2,1)} async-done(((bf16[48,3072]{1,0:T(8,128)(2,1)}), bf16[768,3072]{1,0:T(8,128)(2,1)}) %all-gather.13.cloned.1.call-update) | async-done | bytes 4718608 | tf_op jit(solution)/shard_map/all_gather | solution.py:81
  226.5 7.1 %fusion.67 = f32[512,3072]{1,0:T(8,128)} fusion(bf16[768,3072]{1,0:T(8,128)(2,1)} %all-gather.13.cloned.1.call-done, f32[512,768]{1,0:T(8,128)S(1)} %get-tuple-element.559, f32[768]{0:T(1024)S(1)} %convert_element_type.214, f32[768]{0:T(1024)S(1)} %convert_element_type.213, f32[512]{0:T(512)S(1)} %fusion.61, f32[512]{0:T(512)S(1)} %broadcast_multiply_fusion), kind=kOutput, calls=%fused_computation.108 | convolution fusion | flops 2417885184 | bytes 12593152 | tf_op jit(solution)/shard_map/dot_general | solution.py:165
  233.6 46.8 %all-gather.15.cloned.1.call-done = bf16[3072,768]{1,0:T(8,128)(2,1)} async-done(((bf16[192,768]{1,0:T(8,128)(2,1)}), bf16[3072,768]{1,0:T(8,128)(2,1)}) %all-gather.15.cloned.1.call-update) | async-done | bytes 4718608 | tf_op jit(solution)/shard_map/all_gather | solution.py:83
  280.4 9.3 %fusion.77 = (bf16[3072]{0:T(1024)(128)(2,1)S(1)}, bf16[512,3072]{1,0:T(8,128)(2,1)S(1)}) fusion(f32[512,3072]{1,0:T(8,128)} %fusion.67, f32[3072]{0:T(1024)S(1)} %convert_element_type.216, bf16[3072,768]{1,0:T(8,128)(2,1)} %all-gather.15.cloned.1.call-done, bf16[1,512,768]{2,1,0:T(8,128)(2,1)S(1)} %copy-done.2), kind=kOutput, calls=%fused_computation.117 | convolution fusion | flops 2450519040 | bytes 14960640 | tf_op jit(solution)/shard_map/td,fd->tf/dot_general | solution.py:184
  297.9 7.5 %convolution_convert_fusion.1 = bf16[768,3072]{1,0:T(8,128)(2,1)} fusion(bf16[512,3072]{1,0:T(8,128)(2,1)} %copy-done.22, f32[512,768]{1,0:T(8,128)} %copy-done.4, f32[768]{0:T(1024)S(1)} %convert_element_type.214, f32[768]{0:T(1024)S(1)} %convert_element_type.213, f32[512]{0:T(512)S(1)} %fusion.61, f32[512]{0:T(512)S(1)} %broadcast_multiply_fusion), kind=kOutput, calls=%fused_computation.51 | convolution fusion | flops 2420244480 | bytes 9447424 | tf_op jit(solution)/shard_map/td,tf->df/dot_general | solution.py:186
  305.4 8.7 %convolution_convert_fusion = bf16[3072,768]{1,0:T(8,128)(2,1)} fusion(bf16[1,512,768]{2,1,0:T(8,128)(2,1)S(1)} %copy-done.2, f32[512,3072]{1,0:T(8,128)} %fusion.67, f32[3072]{0:T(1024)S(1)} %convert_element_type.216), kind=kOutput, calls=%fused_computation.50 | convolution fusion | flops 2434007040 | bytes 11808768 | tf_op jit(solution)/shard_map/tf,td->fd/dot_general | solution.py:182
  321.3 173.5 %while.39 = (s32[]{:T(128)}, bf16[512,768]{0,1:T(8,128)(2,1)}, bf16[1024,1536]{0,1:T(8,128)(2,1)}, bf16[1024,1536]{0,1:T(8,128)(2,1)}, bf16[512,768]{0,1:T(8,128...) while((s32[]{:T(128)}, bf16[512,768]{0,1:T(8,128)(2,1)}, ...), condition=%wide.region_12.13_spmd.clone, body=%wide.region_10.12_spmd.clone.sunk | while | flops 686297088 | bytes 35539284 | solution.py:245
  330.9 7.1 %fusion.141 = bf16[2,64,1024]{2,1,0:T(8,128)(2,1)S(1)} fusion(bf16[512,2,64]{0,2,1:T(8,128)(2,1)S(1)} %bitcast.157, f32[2,512,1024]{2,1,0:T(8,128)} %subtract_exponential_fusion.3, f32[2,512,1024]{2,1,0:T(8,128)} %fusion.139), kind=kOutput, calls=%fused_computation.21.clone.1 | convolution fusion | flops 139462656 | bytes 8781824 | tf_op jit(solution)/shard_map/while/body/eval_jaxpr/hts,thd->shd/dot_general | solution.py:222
  342.2 7.2 %fusion.140 = bf16[2,64,512]{2,1,0:T(8,128)(2,1)S(1)} fusion(bf16[1024,2,64]{0,2,1:T(8,128)(2,1)S(1)} %bitcast.152, f32[2,512,1024]{2,1,0:T(8,128)} %subtract_exponential_fusion.3, f32[2,512,1024]{2,1,0:T(8,128)} %fusion.139), kind=kOutput, calls=%fused_computation.22.clone.1 | convolution fusion | flops 139462656 | bytes 8781824 | tf_op jit(solution)/shard_map/while/body/eval_jaxpr/hts,shd->thd/dot_general | solution.py:219
  359.5 7.3 %fusion.141 = bf16[2,64,1024]{2,1,0:T(8,128)(2,1)S(1)} fusion(bf16[512,2,64]{0,2,1:T(8,128)(2,1)S(1)} %bitcast.157, f32[2,512,1024]{2,1,0:T(8,128)} %subtract_exponential_fusion.3, f32[2,512,1024]{2,1,0:T(8,128)} %fusion.139), kind=kOutput, calls=%fused_computation.21.clone.1 | convolution fusion | flops 139462656 | bytes 8781824 | tf_op jit(solution)/shard_map/while/body/eval_jaxpr/hts,thd->shd/dot_general | solution.py:222
  371.1 7.9 %fusion.140 = bf16[2,64,512]{2,1,0:T(8,128)(2,1)S(1)} fusion(bf16[1024,2,64]{0,2,1:T(8,128)(2,1)S(1)} %bitcast.152, f32[2,512,1024]{2,1,0:T(8,128)} %subtract_exponential_fusion.3, f32[2,512,1024]{2,1,0:T(8,128)} %fusion.139), kind=kOutput, calls=%fused_computation.22.clone.1 | convolution fusion | flops 139462656 | bytes 8781824 | tf_op jit(solution)/shard_map/while/body/eval_jaxpr/hts,shd->thd/dot_general | solution.py:219
  389.1 7.1 %fusion.141 = bf16[2,64,1024]{2,1,0:T(8,128)(2,1)S(1)} fusion(bf16[512,2,64]{0,2,1:T(8,128)(2,1)S(1)} %bitcast.157, f32[2,512,1024]{2,1,0:T(8,128)} %subtract_exponential_fusion.3, f32[2,512,1024]{2,1,0:T(8,128)} %fusion.139), kind=kOutput, calls=%fused_computation.21.clone.1 | convolution fusion | flops 139462656 | bytes 8781824 | tf_op jit(solution)/shard_map/while/body/eval_jaxpr/hts,thd->shd/dot_general | solution.py:222
  400.4 7.2 %fusion.140 = bf16[2,64,512]{2,1,0:T(8,128)(2,1)S(1)} fusion(bf16[1024,2,64]{0,2,1:T(8,128)(2,1)S(1)} %bitcast.152, f32[2,512,1024]{2,1,0:T(8,128)} %subtract_exponential_fusion.3, f32[2,512,1024]{2,1,0:T(8,128)} %fusion.139), kind=kOutput, calls=%fused_computation.22.clone.1 | convolution fusion | flops 139462656 | bytes 8781824 | tf_op jit(solution)/shard_map/while/body/eval_jaxpr/hts,shd->thd/dot_general | solution.py:219
  417.7 7.1 %fusion.141 = bf16[2,64,1024]{2,1,0:T(8,128)(2,1)S(1)} fusion(bf16[512,2,64]{0,2,1:T(8,128)(2,1)S(1)} %bitcast.157, f32[2,512,1024]{2,1,0:T(8,128)} %subtract_exponential_fusion.3, f32[2,512,1024]{2,1,0:T(8,128)} %fusion.139), kind=kOutput, calls=%fused_computation.21.clone.1 | convolution fusion | flops 139462656 | bytes 8781824 | tf_op jit(solution)/shard_map/while/body/eval_jaxpr/hts,thd->shd/dot_general | solution.py:222
  429.0 7.2 %fusion.140 = bf16[2,64,512]{2,1,0:T(8,128)(2,1)S(1)} fusion(bf16[1024,2,64]{0,2,1:T(8,128)(2,1)S(1)} %bitcast.152, f32[2,512,1024]{2,1,0:T(8,128)} %subtract_exponential_fusion.3, f32[2,512,1024]{2,1,0:T(8,128)} %fusion.139), kind=kOutput, calls=%fused_computation.22.clone.1 | convolution fusion | flops 139462656 | bytes 8781824 | tf_op jit(solution)/shard_map/while/body/eval_jaxpr/hts,shd->thd/dot_general | solution.py:219
  446.2 7.8 %fusion.141 = bf16[2,64,1024]{2,1,0:T(8,128)(2,1)S(1)} fusion(bf16[512,2,64]{0,2,1:T(8,128)(2,1)S(1)} %bitcast.157, f32[2,512,1024]{2,1,0:T(8,128)} %subtract_exponential_fusion.3, f32[2,512,1024]{2,1,0:T(8,128)} %fusion.139), kind=kOutput, calls=%fused_computation.21.clone.1 | convolution fusion | flops 139462656 | bytes 8781824 | tf_op jit(solution)/shard_map/while/body/eval_jaxpr/hts,thd->shd/dot_general | solution.py:222
  458.3 7.2 %fusion.140 = bf16[2,64,512]{2,1,0:T(8,128)(2,1)S(1)} fusion(bf16[1024,2,64]{0,2,1:T(8,128)(2,1)S(1)} %bitcast.152, f32[2,512,1024]{2,1,0:T(8,128)} %subtract_exponential_fusion.3, f32[2,512,1024]{2,1,0:T(8,128)} %fusion.139), kind=kOutput, calls=%fused_computation.22.clone.1 | convolution fusion | flops 139462656 | bytes 8781824 | tf_op jit(solution)/shard_map/while/body/eval_jaxpr/hts,shd->thd/dot_general | solution.py:219
  475.6 7.1 %fusion.141 = bf16[2,64,1024]{2,1,0:T(8,128)(2,1)S(1)} fusion(bf16[512,2,64]{0,2,1:T(8,128)(2,1)S(1)} %bitcast.157, f32[2,512,1024]{2,1,0:T(8,128)} %subtract_exponential_fusion.3, f32[2,512,1024]{2,1,0:T(8,128)} %fusion.139), kind=kOutput, calls=%fused_computation.21.clone.1 | convolution fusion | flops 139462656 | bytes 8781824 | tf_op jit(solution)/shard_map/while/body/eval_jaxpr/hts,thd->shd/dot_general | solution.py:222
  487.0 7.2 %fusion.140 = bf16[2,64,512]{2,1,0:T(8,128)(2,1)S(1)} fusion(bf16[1024,2,64]{0,2,1:T(8,128)(2,1)S(1)} %bitcast.152, f32[2,512,1024]{2,1,0:T(8,128)} %subtract_exponential_fusion.3, f32[2,512,1024]{2,1,0:T(8,128)} %fusion.139), kind=kOutput, calls=%fused_computation.22.clone.1 | convolution fusion | flops 139462656 | bytes 8781824 | tf_op jit(solution)/shard_map/while/body/eval_jaxpr/hts,shd->thd/dot_general | solution.py:219
  495.0 17.0 %reduce-scatter.14.cloned.1.call-done = bf16[192,768]{1,0:T(8,128)(2,1)} async-done(((bf16[3072,768]{1,0:T(8,128)(2,1)}), bf16[192,768]{1,0:T(8,128)(2,1)}) %reduce-scatter.14.cloned.1.call-update) | async-done | bytes 294928 | tf_op jit(solution)/shard_map/reduce_scatter | solution.py:303
  512.0 44.9 %reduce-scatter.6.cloned.1.call-done = bf16[512,1536]{0,1:T(8,128)(2,1)} async-done(((bf16[1024,1536]{0,1:T(8,128)(2,1)}), bf16[512,1536]{0,1:T(8,128)(2,1)}) %reduce-scatter.6.cloned.1.call-update) | async-done | bytes 1572880 | tf_op jit(solution)/shard_map/reduce_scatter | solution.py:254
  556.9 5.6 convolution_convert_fusion.2
  567.4 5.0 fusion.68
  574.4 61.4 %all-reduce.18 = (bf16[768]{0:T(1024)(128)(2,1)S(1)}, bf16[768]{0:T(1024)(128)(2,1)S(1)}, bf16[768]{0:T(1024)(128)(2,1)S(1)}, bf16[768]{0:T(1024)(128)(2,1)S(1)}...) all-reduce(bf16[768]{0:T(1024)(128)(2,1)S(1)} %dynamic-update-slice, ...), channel_id=1, replica_groups=mesh['dp'=16,'ctx'=2] {'dp'}, use_global_device_ids=true, to_apply=%add.8 | all-reduce | flops 9984 | bytes 39936
  636.5 5.2 all-reduce.20
  649.4 9.0 %fusion.48 = bf16[1,512,768]{2,1,0:T(8,128)(2,1)} fusion(f32[512,768]{1,0:T(8,128)S(1)} %copy-done.5, bf16[3072,768]{1,0:T(8,128)(2,1)} %all-gather.15.cloned.1.call-done, f32[768]{0:T(1024)S(1)} %convert_element_type.218, f32[512,3072]{1,0:T(8,128)} %fusion.67, f32[3072]{0:T(1024)S(1)} %convert_element_type.216), kind=kOutput, calls=%fused_computation.82 | convolution fusion | flops 2432827392 | bytes 13384704 | tf_op jit(solution)/shard_map/dot_general | solution.py:171
  663.6 6.8 %all-gather = bf16[96,2304]{1,0:T(8,128)(2,1)S(1)} all-gather(bf16[48,2304]{1,0:T(8,128)(2,1)} %reduce-scatter.8.cloned.1.call-done), channel_id=2, replica_groups=mesh['dp'=16,'ctx'=2] {'ctx'}, dimensions={0}, use_global_device_ids=true | all-gather | bytes 663552 | tf_op jit(solution)/shard_map/all_gather | solution.py:14
  (291 shorter events, 201.2 us)
Async XLA Ops:
  7.2 76.3 %all-gather.7.cloned.1.call-start = ((), (), s32[]{:S(2)}) async-start(), calls=%async_computation.5 | async-start | bytes 3760128 | tf_op jit(solution)/shard_map/all_gather | solution.py:74
  7.9 123.8 %all-gather.9.cloned.1.call-start = ((), (), s32[]{:S(2)}) async-start(), calls=%async_computation.6 | async-start | bytes 4718592 | tf_op jit(solution)/shard_map/all_gather | solution.py:118
  83.5 4.5 copy-start.13
  88.0 3.8 copy-start.15
  88.0 5.1 copy-start.19
  88.0 6.4 copy-start.16
  88.0 6.4 copy-start.17
  88.0 6.4 copy-start.18
  89.3 103.7 %all-gather.11.cloned.1.call-start = ((), (), s32[]{:S(2)}) async-start(), calls=%async_computation.7 | async-start | bytes 1253376 | tf_op jit(solution)/shard_map/all_gather | solution.py:77
  90.0 136.5 %all-gather.13.cloned.1.call-start = ((), (), s32[]{:S(2)}) async-start(), calls=%async_computation.8 | async-start | bytes 5013504 | tf_op jit(solution)/shard_map/all_gather | solution.py:81
  90.6 189.8 %all-gather.15.cloned.1.call-start = ((), (), s32[]{:S(2)}) async-start(), calls=%async_computation.9 | async-start | bytes 5013504 | tf_op jit(solution)/shard_map/all_gather | solution.py:83
  91.2 403.7 %reduce-scatter.10.cloned.1.call-start = ((), (), s32[]{:S(2)}) async-start(), calls=%async_computation.12 | async-start | bytes 1253376 | tf_op jit(solution)/shard_map/reduce_scatter | solution.py:285
  136.5 57.3 %copy-start.1 = (bf16[1,512,768]{2,1,0:T(8,128)(2,1)S(1)}, bf16[1,512,768]{2,1,0:T(8,128)(2,1)}, u32[]{:S(2)}) copy-start(bf16[1,512,768]{2,1,0:T(8,128)(2,1)} %param.24) | copy-start | bytes 2359300
  148.5 1.9 copy-start
  157.8 1.9 copy-start
  167.2 1.9 copy-start
  186.1 1.9 copy-start
  192.9 3.4 copy-start.9
  196.0 93.7 %copy-start.4 = (f32[512,768]{1,0:T(8,128)}, f32[512,768]{1,0:T(8,128)S(1)}, u32[]{:S(2)}) copy-start(f32[512,768]{1,0:T(8,128)S(1)} %get-tuple-element.559) | copy-start | bytes 4718596
  196.3 84.0 %copy-start.2 = (bf16[1,512,768]{2,1,0:T(8,128)(2,1)S(1)}, bf16[1,512,768]{2,1,0:T(8,128)(2,1)}, u32[]{:S(2)}) copy-start(bf16[1,512,768]{2,1,0:T(8,128)(2,1)} %param.39) | copy-start | bytes 2359300
  280.4 9.4 %copy-start.20 = (bf16[768,3072]{1,0:T(8,128)(2,1)S(1)}, bf16[768,3072]{1,0:T(8,128)(2,1)}, u32[]{:S(2)}) copy-start(bf16[768,3072]{1,0:T(8,128)(2,1)} %all-gather.13.cloned.1.call-done) | copy-start | bytes 14155780
  289.7 3.0 copy-start.22
  292.7 3.3 copy-start.10
  297.9 197.1 %reduce-scatter.12.cloned.1.call-start = ((), (), s32[]{:S(2)}) async-start(), calls=%async_computation.13 | async-start | bytes 5013504 | tf_op jit(solution)/shard_map/reduce_scatter | solution.py:297
  305.4 206.6 %reduce-scatter.14.cloned.1.call-start = ((), (), s32[]{:S(2)}) async-start(), calls=%async_computation.14 | async-start | bytes 5013504 | tf_op jit(solution)/shard_map/reduce_scatter | solution.py:303
  314.1 242.8 %reduce-scatter.6.cloned.1.call-start = ((), (), s32[]{:S(2)}) async-start(), calls=%async_computation.10 | async-start | bytes 4718592 | tf_op jit(solution)/shard_map/reduce_scatter | solution.py:254
  494.8 62.1 %copy-start.8 = (bf16[512,768]{0,1:T(8,128)(2,1)S(1)}, bf16[512,768]{0,1:T(8,128)(2,1)}, u32[]{:S(2)}) copy-start(bf16[512,768]{0,1:T(8,128)(2,1)} %get-tuple-element.395) | copy-start | bytes 2359300
  494.9 163.5 %all-reduce.24.cloned.1.call-start = ((), (), s32[]{:S(2)}) async-start(), calls=%async_computation.15 | async-start | bytes 1327104 | tf_op jit(solution)/shard_map/psum | solution.py:331
  512.0 151.6 %reduce-scatter.8.cloned.1.call-start = ((), (), s32[]{:S(2)}) async-start(), calls=%async_computation.11 | async-start | bytes 3760128 | tf_op jit(solution)/shard_map/reduce_scatter | solution.py:276
  562.5 2.6 copy-start.21
  567.4 5.1 copy-start.14
  641.7 7.7 %copy-start.5 = (f32[512,768]{1,0:T(8,128)S(1)}, f32[512,768]{1,0:T(8,128)}, u32[]{:S(2)}) copy-start(f32[512,768]{1,0:T(8,128)} %copy-done.4) | copy-start | bytes 4718596
  (7 other events, 9.1 us)
Sparse Core Ops, SparseCore 0:
  10.3 50.2 all-gather.6
  89.4 42.2 all-gather.8
  134.0 38.2 all-gather.10
  174.5 51.9 all-gather.12
  228.7 51.6 all-gather.14
  298.0 56.7 reduce-scatter.9
  358.7 74.5 reduce-scatter.11
  437.1 74.8 reduce-scatter.13
  514.2 42.6 reduce-scatter.5
  559.2 31.7 all-reduce.23
  594.9 68.4 reduce-scatter.7
